TPU v7x, 32 devices: a whole 2x2x4 slice. The times are simulated.
32 devices in a mesh: lat: 4 (over y, x), lon: 8 (over z, core).
Axes of the slice: x: 2, y: 2, z: 4, core: 2. Of those that a mesh axis runs over, the one named last changes fastest.
Arguments:
- right_side: float32 [8, 768, 1024], P(None, 'lat', 'lon'), may hold values from -16 to 16
- center: float32 [768, 1024], P('lat', 'lon'), may hold values from 3.7 to 5.5
- couplings: float32 [4, 768, 1024], P(None, 'lat', 'lon'), may hold values from 0.15 to 0.45
- land_sea: int32 [768, 1024], P('lat', 'lon'), may hold values 0 or 1
- fold_partner: int32 [1024], replicated, may hold values from 0 to 1023, as said below
Outputs:
- solution: float32 [8, 768, 1024], P(None, 'lat', 'lon')
- residual: float32 [8, 768, 1024], P(None, 'lat', 'lon')
Inputs may be any that keep to these rules, and one draw needn't show every extreme that they name: fold_partner[i] = (s - i) mod 1024 for one integer s, so fold_partner[fold_partner[i]] = i.
All inputs are finite; a program needn't handle non-finite values. No bound on the sum of `land_sea` on one device may be relied on, other than what follows from the above.
Results may differ from a plain program's by a relative error of at most 0.0003.
Values sent between devices are 32-bit elements; how exact they have to be, the bound alone decides.
No kernel may reach another device: no remote copies, remote signals or barrier semaphores. Data moves between devices by JAX's collectives and lax.ppermute only.
A program may use at most 64 MiB of HBM per device.

v0:
```python
import jax
import jax.numpy as jnp
from jax import lax
from jax.sharding import PartitionSpec as P

ITERS = 3


def extended(cells, sides, width, closed):
    for axis, dim in sides:
        count = lax.axis_size(axis)
        ends = count if closed else count - 1
        head = lax.slice_in_dim(cells, 0, width, axis=dim)
        tail = lax.slice_in_dim(cells, cells.shape[dim] - width, cells.shape[dim], axis=dim)
        cells = jnp.concatenate(
            [
                lax.ppermute(tail, axis, [(i, (i + 1) % count) for i in range(ends)]),
                cells,
                lax.ppermute(head, axis, [((i + 1) % count, i) for i in range(ends)]),
            ],
            axis=dim,
        )
    return cells


def body(right_side, center, couplings, land_sea, fold_partner):
    row_count, col_count = center.shape
    lat_last = lax.axis_index("lat") == lax.axis_size("lat") - 1
    lat_first = lax.axis_index("lat") == 0
    first_col = lax.axis_index("lon") * col_count
    partner_local = lax.dynamic_slice_in_dim(fold_partner, first_col, col_count, 0)
    ocean_mask = land_sea.astype(jnp.float32)
    north_top = couplings[1, -1, :]
    whole_north = lax.all_gather(north_top, "lon", axis=0, tiled=True)
    fold_coeff = 0.5 * (north_top + jnp.take(whole_north, partner_local, axis=0))
    row_index = lax.broadcasted_iota(jnp.int32, (row_count, col_count), 0)
    top_rows = jnp.logical_and(lat_last, row_index == row_count - 1)
    east_coeff = couplings[0]
    north_coeff = jnp.where(top_rows, fold_coeff[None, :], couplings[1])
    northeast = jnp.where(top_rows, 0.0, couplings[2])
    northwest = jnp.where(top_rows, 0.0, couplings[3])
    stacked = jnp.stack([east_coeff, north_coeff, northeast, northwest])
    coeff_padded = extended(stacked, (("lat", 1), ("lon", 2)), 1, True)
    ghost_rows = lax.broadcasted_iota(jnp.int32, (1, row_count + 2, col_count + 2), 1)
    coeff_padded = jnp.where(jnp.logical_and(lat_first, ghost_rows == 0), 0.0, coeff_padded)
    west_coeff = coeff_padded[0, 1:-1, :-2]
    south_coeff = coeff_padded[1, :-2, 1:-1]
    southwest = coeff_padded[2, :-2, :-2]
    southeast = coeff_padded[3, :-2, 2:]

    def operate(vector):
        top_row = vector[:, -1, :]
        whole_top = lax.all_gather(top_row, "lon", axis=1, tiled=True)
        fold_ghost = jnp.take(whole_top, partner_local, axis=1)
        lon_padded = extended(vector, (("lon", 2),), 1, True)
        padded = extended(lon_padded, (("lat", 1),), 1, False)
        north_row = jnp.where(lat_last, fold_ghost, padded[:, -1, 1:-1])
        padded = padded.at[:, -1, 1:-1].set(north_row)
        upper = padded[:, 2:, 1:-1]
        lower = padded[:, :-2, 1:-1]
        beside = east_coeff * padded[:, 1:-1, 2:] + west_coeff * padded[:, 1:-1, :-2]
        beside = beside + north_coeff * upper + south_coeff * lower
        beside = beside + northeast * padded[:, 2:, 2:] + southwest * padded[:, :-2, :-2]
        beside = beside + northwest * padded[:, 2:, :-2] + southeast * padded[:, :-2, 2:]
        return ocean_mask * (center * vector - beside)

    def paired_sums(residual, scaled, image):
        return lax.psum(
            (jnp.sum(residual * scaled, axis=(1, 2)), jnp.sum(scaled * image, axis=(1, 2))),
            ("lat", "lon"),
        )

    residual = right_side * ocean_mask
    solution = jnp.zeros_like(residual)
    scaled = residual / center
    image = operate(scaled)
    gamma_now, curve = paired_sums(residual, scaled, image)
    step_size = gamma_now / curve
    direction = scaled
    along_dir = image
    for iteration in range(ITERS):
        solution = solution + step_size[:, None, None] * direction
        residual = residual - step_size[:, None, None] * along_dir
        if iteration + 1 < ITERS:
            scaled = residual / center
            image = operate(scaled)
            gamma_next, curve = paired_sums(residual, scaled, image)
            beta_ratio = gamma_next / gamma_now
            step_size = gamma_next / (curve - beta_ratio * gamma_next / step_size)
            direction = scaled + beta_ratio[:, None, None] * direction
            along_dir = image + beta_ratio[:, None, None] * along_dir
            gamma_now = gamma_next
    return (solution, residual)


def solution(mesh):
    return jax.shard_map(
        body,
        mesh=mesh,
        in_specs=(
            P(None, "lat", "lon"),
            P("lat", "lon"),
            P(None, "lat", "lon"),
            P("lat", "lon"),
            P(),
        ),
        out_specs=(P(None, "lat", "lon"), P(None, "lat", "lon")),
        check_vma=False,
    )
```

profile of v0, /device:TPU:0, one launch (start us, length us, event | category | flops | bytes accessed | tf_op | source)
XLA Modules:
  0.0 254.5 jit_solution(16460176406055515500)
XLA Ops:
  1.4 13.4 %all-gather.1 = f32[1,1,1024]{2,1,0:T(1,128)S(1)} all-gather(f32[1,1,128]{2,1,0:T(1,128)S(1)} %slice.247), channel_id=3, replica_groups=mesh['lat'=4,'lon'=8] {'lon'}, dimensions={2}, use_global_device_ids=true | all-gather | bytes 4608 | tf_op jit(solution)/shard_map/all_gather | solution.py:34
  17.3 1.7 slice_select_fusion.2
  19.0 1.5 collective-permute-start.4
  20.6 1.4 collective-permute-start.5
  23.3 1.5 copy.91
  27.7 2.5 collective-permute-start.7
  30.2 13.8 %all-gather = f32[8,1,1024]{2,1,0:T(1,128)S(1)} all-gather(f32[8,1,128]{2,1,0:T(1,128)S(1)} %slice.304), channel_id=2, replica_groups=mesh['lat'=4,'lon'=8] {'lon'}, dimensions={2}, use_global_device_ids=true | all-gather | bytes 36864 | tf_op jit(solution)/shard_map/all_gather | solution.py:53
  45.4 2.4 maximum_select_fusion
  48.5 2.5 collective-permute-start.2
  52.3 2.0 slice_bitcast_fusion.3
  54.3 2.7 %collective-permute-done.3 = f32[8,1,130]{2,0,1:T(8,128)S(1)} collective-permute-done((f32[8,1,130]{2,0,1:T(8,128)S(1)}, f32[8,1,130]{2,0,1:T(8,128)S(1)}, u32[]{:S(2)}, u32[]{:S(2)}) %collective-permute-start.3) | collective-permute-done | bytes 4192 | tf_op jit(solution)/shard_map/ppermute | solution.py:19
  58.2 1.3 scatter.10
  59.6 2.5 multiply_reduce_fusion.4
  62.1 39.8 %all-reduce.2 = (f32[8]{0:T(128)S(1)}, f32[8]{0:T(128)S(1)}) all-reduce(f32[8]{0:T(128)S(1)} %get-tuple-element.50, f32[8]{0:T(128)S(1)} %get-tuple-element.49), channel_id=1, replica_groups=mesh['lat'=4,'lon'=8] {'lat','lon'}, use_global_device_ids=true, to_apply=%region_1.2 | all-reduce | flops 16 | bytes 128 | tf_op jit(solution)/shard_map/psum | solution.py:68
  101.9 2.0 broadcast_divide_fusion.1
  104.9 3.5 %collective-permute-start.9 = (f32[8,192,1]{1,0,2:T(8,128)S(1)}, f32[8,192,1]{1,0,2:T(8,128)S(1)}, u32[]{:S(2)}, u32[]{:S(2)}) collective-permute-start(f32[8,192,1]{1,0,2:T(8,128)S(1)} %copy.100), channel_id=1, source_target_pairs={{1,0},{2,1},{3,2},{4,3},{5,4},{6,5},{7,6},{0,7},{9,8},{10,9},{11,1... | collective-permute-start | bytes 18440 | tf_op jit(solution)/shard_map/ppermute | solution.py:19
  111.6 4.8 %collective-permute-start.10 = (f32[8,1,130]{2,0,1:T(8,128)S(1)}, f32[8,1,130]{2,0,1:T(8,128)S(1)}, u32[]{:S(2)}, u32[]{:S(2)}) collective-permute-start(f32[8,1,130]{2,0,1:T(8,128)S(1)} %copy.103), channel_id=1, source_target_pairs={{0,8},{8,16},{16,24},{1,9},{9,17},{17,25},{2,10},{10,18},{18,26},{... | collective-permute-start | bytes 12488 | tf_op jit(solution)/shard_map/ppermute | solution.py:17
  116.4 9.9 %all-gather.2 = f32[8,1,1024]{2,1,0:T(1,128)S(1)} all-gather(f32[8,1,128]{2,1,0:T(1,128)S(1)} %slice.322), channel_id=4, replica_groups=mesh['lat'=4,'lon'=8] {'lon'}, dimensions={2}, use_global_device_ids=true | all-gather | bytes 36864 | tf_op jit(solution)/shard_map/all_gather | solution.py:53
  127.3 1.7 gather_fusion.2
  129.2 2.1 pad_maximum_fusion
  131.3 1.3 scatter.11
  132.7 3.4 %multiply_reduce_fusion.2 = (f32[8]{0:T(128)S(1)}, f32[8]{0:T(128)S(1)}, f32[8,192,128]{2,1,0:T(8,128)}) fusion(f32[8,192,128]{2,1,0:T(8,128)} %get-tuple-element.71, f32[192,128]{1,0:T(8,128)} %param.14, f32[8,194,130]{2,1,0:T(8,128)S(1)} %scatter.11, f32[192,128]{1,0:T(8,128)} %get-tuple-element.82, f32[192,128]{1,0:T(8,128)S(1)} %bitcast.51, ...), kind=kLoop, calls=%fused_computation.65 | loop fusion | flops 4521968 | bytes 8847424 | tf_op jit(solution)/shard_map/reduce_sum | solution.py:69
  136.0 39.6 %all-reduce.1 = (f32[8]{0:T(128)S(1)}, f32[8]{0:T(128)S(1)}) all-reduce(f32[8]{0:T(128)S(1)} %get-tuple-element.54, f32[8]{0:T(128)S(1)} %get-tuple-element.53), channel_id=1, replica_groups=mesh['lat'=4,'lon'=8] {'lat','lon'}, use_global_device_ids=true, to_apply=%region_5.7 | all-reduce | flops 16 | bytes 128 | tf_op jit(solution)/shard_map/psum | solution.py:68
  176.2 2.8 %broadcast_divide_fusion = (f32[8,192,128]{2,1,0:T(8,128)S(1)}, f32[8,192,128]{2,1,0:T(8,128)}) fusion(f32[192,128]{1,0:T(8,128)} %param.14, f32[8,192,128]{2,1,0:T(8,128)} %get-tuple-element.71, f32[8,192,128]{2,1,0:T(8,128)} %get-tuple-element.69, f32[8,192,128]{2,1,0:T(8,128)} %copy-done.1, f32[8]{0:T(128)S(1)} %get-tuple-element.68, ...), kind=kLoop, calls=%fused_computation.72 | loop fusion | flops 983040 | bytes 4030528 | tf_op jit(solution)/shard_map/div | solution.py:85
  180.1 3.5 %collective-permute-start.13 = (f32[8,192,1]{1,0,2:T(8,128)S(1)}, f32[8,192,1]{1,0,2:T(8,128)S(1)}, u32[]{:S(2)}, u32[]{:S(2)}) collective-permute-start(f32[8,192,1]{1,0,2:T(8,128)S(1)} %copy.110), channel_id=1, source_target_pairs={{1,0},{2,1},{3,2},{4,3},{5,4},{6,5},{7,6},{0,7},{9,8},{10,9},{11,1... | collective-permute-start | bytes 18440 | tf_op jit(solution)/shard_map/ppermute | solution.py:19
  186.7 4.8 %collective-permute-start.14 = (f32[8,1,130]{2,0,1:T(8,128)S(1)}, f32[8,1,130]{2,0,1:T(8,128)S(1)}, u32[]{:S(2)}, u32[]{:S(2)}) collective-permute-start(f32[8,1,130]{2,0,1:T(8,128)S(1)} %copy.113), channel_id=1, source_target_pairs={{0,8},{8,16},{16,24},{1,9},{9,17},{17,25},{2,10},{10,18},{18,26},{... | collective-permute-start | bytes 12488 | tf_op jit(solution)/shard_map/ppermute | solution.py:17
  191.6 9.9 %all-gather.3 = f32[8,1,1024]{2,1,0:T(1,128)S(1)} all-gather(f32[8,1,128]{2,1,0:T(1,128)S(1)} %slice.334), channel_id=5, replica_groups=mesh['lat'=4,'lon'=8] {'lon'}, dimensions={2}, use_global_device_ids=true | all-gather | bytes 36864 | tf_op jit(solution)/shard_map/all_gather | solution.py:53
  202.5 1.7 gather_fusion.3
  204.3 2.1 pad_maximum_fusion.1
  207.9 3.5 %multiply_reduce_fusion = (f32[8]{0:T(128)S(1)}, f32[8]{0:T(128)S(1)}, f32[8,192,128]{2,1,0:T(8,128)}) fusion(f32[8,192,128]{2,1,0:T(8,128)} %get-tuple-element.65, f32[192,128]{1,0:T(8,128)} %param.14, f32[8,194,130]{2,1,0:T(8,128)S(1)} %scatter.14, f32[192,128]{1,0:T(8,128)} %get-tuple-element.82, f32[192,128]{1,0:T(8,128)S(1)} %bitcast.52, ...), kind=kLoop, calls=%fused_computation.61 | loop fusion | flops 4521968 | bytes 8847424 | tf_op jit(solution)/shard_map/reduce_sum | solution.py:69
  211.4 39.4 %all-reduce = (f32[8]{0:T(128)S(1)}, f32[8]{0:T(128)S(1)}) all-reduce(f32[8]{0:T(128)S(1)} %get-tuple-element.52, f32[8]{0:T(128)S(1)} %get-tuple-element.51), channel_id=1, replica_groups=mesh['lat'=4,'lon'=8] {'lat','lon'}, use_global_device_ids=true, to_apply=%region_9.11 | all-reduce | flops 16 | bytes 128 | tf_op jit(solution)/shard_map/psum | solution.py:68
  250.8 3.7 %multiply_subtract_fusion = (f32[8,192,128]{2,1,0:T(8,128)}, f32[8,192,128]{2,1,0:T(8,128)}) fusion(f32[8,192,128]{2,1,0:T(8,128)} %get-tuple-element.65, f32[8,192,128]{2,1,0:T(8,128)} %get-tuple-element.63, f32[8]{0:T(128)S(1)} %get-tuple-element.62, f32[8]{0:T(128)S(1)} %get-tuple-element.61, f32[8,192,128]{2,1,0:T(8,128)} %get-tuple-element.69, ...), kind=kLoop, calls=%fused_computation.59 | loop fusion | flops 3735552 | bytes 6488224 | tf_op jit(solution)/shard_map/sub | solution.py:83
  (122 shorter events, 24.5 us)
Async XLA Ops:
  0.6 21.4 %copy-start.9 = (s32[192,128]{1,0:T(8,128)S(1)}, s32[192,128]{1,0:T(8,128)}, u32[]{:S(2)}) copy-start(s32[192,128]{1,0:T(8,128)} %param.16) | copy-start | bytes 294916
  0.6 21.4 %copy-start.8 = (f32[192,128]{1,0:T(8,128)S(1)}, f32[192,128]{1,0:T(8,128)}, u32[]{:S(2)}) copy-start(f32[192,128]{1,0:T(8,128)} %param.14) | copy-start | bytes 294916
  0.7 21.4 %copy-start = (f32[8,192,128]{2,1,0:T(8,128)S(1)}, f32[8,192,128]{2,1,0:T(8,128)}, u32[]{:S(2)}) copy-start(f32[8,192,128]{2,1,0:T(8,128)} %param.13) | copy-start | bytes 2359300
  19.0 26.3 %copy-start.7 = (f32[1,192,128]{2,1,0:T(8,128)}, f32[1,192,128]{2,1,0:T(8,128)S(1)}, u32[]{:S(2)}) copy-start(f32[1,192,128]{2,1,0:T(8,128)S(1)} %get-tuple-element.97) | copy-start | bytes 294916
  19.0 6.6 %collective-permute-start.4 = (f32[4,1,128]{2,1,0:T(1,128)S(1)}, f32[4,1,128]{2,1,0:T(1,128)S(1)}, u32[]{:S(2)}, u32[]{:S(2)}) collective-permute-start(f32[4,1,128]{2,1,0:T(1,128)S(1)} %get-tuple-element.99), channel_id=1, source_target_pairs={{0,8},{8,16},{16,24},{24,0},{1,9},{9,17},{17,25},{25,1},{2,10},{10... | collective-permute-start | bytes 6152 | tf_op jit(solution)/shard_map/ppermute | solution.py:17
  20.6 5.0 %collective-permute-start.5 = (f32[4,1,128]{2,1,0:T(1,128)S(1)}, f32[4,1,128]{2,1,0:T(1,128)S(1)}, u32[]{:S(2)}, u32[]{:S(2)}) collective-permute-start(f32[4,1,128]{2,1,0:T(1,128)S(1)} %get-tuple-element.100), channel_id=1, source_target_pairs={{8,0},{16,8},{24,16},{0,24},{9,1},{17,9},{25,17},{1,25},{10,2},{18... | collective-permute-start | bytes 6152 | tf_op jit(solution)/shard_map/ppermute | solution.py:19
  24.7 23.4 %collective-permute-start.1 = (f32[8,192,1]{1,0,2:T(8,128)S(1)}, f32[8,192,1]{1,0,2:T(8,128)S(1)}, u32[]{:S(2)}, u32[]{:S(2)}) collective-permute-start(f32[8,192,1]{1,0,2:T(8,128)S(1)} %copy.91), channel_id=1, source_target_pairs={{1,0},{2,1},{3,2},{4,3},{5,4},{6,5},{7,6},{0,7},{9,8},{10,9},{11,1... | collective-permute-start | bytes 18440 | tf_op jit(solution)/shard_map/ppermute | solution.py:19
  25.1 22.7 %collective-permute-start = (f32[8,192,1]{1,0,2:T(8,128)S(1)}, f32[8,192,1]{1,0,2:T(8,128)S(1)}, u32[]{:S(2)}, u32[]{:S(2)}) collective-permute-start(f32[8,192,1]{1,0,2:T(8,128)S(1)} %copy.90), channel_id=1, source_target_pairs={{0,1},{1,2},{2,3},{3,4},{4,5},{5,6},{6,7},{7,0},{8,9},{9,10},{10,1... | collective-permute-start | bytes 18440 | tf_op jit(solution)/shard_map/ppermute | solution.py:17
  26.7 18.7 %collective-permute-start.6 = (f32[4,194,1]{2,1,0:T(8,128)}, f32[4,194,1]{2,1,0:T(8,128)S(1)}, u32[]{:S(2)}, u32[]{:S(2)}) collective-permute-start(f32[4,194,1]{2,1,0:T(8,128)} %get-tuple-element.93), channel_id=1, source_target_pairs={{0,1},{1,2},{2,3},{3,4},{4,5},{5,6},{6,7},{7,0},{8,9},{9,10},{10,1... | collective-permute-start | bytes 9320 | tf_op jit(solution)/shard_map/ppermute | solution.py:17
  27.7 17.7 %collective-permute-start.7 = (f32[4,194,1]{2,1,0:T(8,128)}, f32[4,194,1]{2,1,0:T(8,128)}, u32[]{:S(2)}, u32[]{:S(2)}) collective-permute-start(f32[4,194,1]{2,1,0:T(8,128)} %get-tuple-element.94), channel_id=1, source_target_pairs={{1,0},{2,1},{3,2},{4,3},{5,4},{6,5},{7,6},{0,7},{9,8},{10,9},{11,1... | collective-permute-start | bytes 9320 | tf_op jit(solution)/shard_map/ppermute | solution.py:19
  48.5 5.8 %collective-permute-start.2 = (f32[8,1,130]{2,0,1:T(8,128)S(1)}, f32[8,1,130]{2,0,1:T(8,128)S(1)}, u32[]{:S(2)}, u32[]{:S(2)}) collective-permute-start(f32[8,1,130]{2,0,1:T(8,128)S(1)} %get-tuple-element.79), channel_id=1, source_target_pairs={{0,8},{8,16},{16,24},{1,9},{9,17},{17,25},{2,10},{10,18},{18,26},{... | collective-permute-start | bytes 12488 | tf_op jit(solution)/shard_map/ppermute | solution.py:17
  51.0 5.9 %collective-permute-start.3 = (f32[8,1,130]{2,0,1:T(8,128)S(1)}, f32[8,1,130]{2,0,1:T(8,128)S(1)}, u32[]{:S(2)}, u32[]{:S(2)}) collective-permute-start(f32[8,1,130]{2,0,1:T(8,128)S(1)} %get-tuple-element.80), channel_id=1, source_target_pairs={{8,0},{16,8},{24,16},{9,1},{17,9},{25,17},{10,2},{18,10},{26,18},{... | collective-permute-start | bytes 12488 | tf_op jit(solution)/shard_map/ppermute | solution.py:19
  62.1 41.8 %copy-start.1 = (f32[8,192,128]{2,1,0:T(8,128)}, f32[8,192,128]{2,1,0:T(8,128)S(1)}, u32[]{:S(2)}) copy-start(f32[8,192,128]{2,1,0:T(8,128)S(1)} %get-tuple-element.72) | copy-start | bytes 2359300
  104.5 4.9 %collective-permute-start.8 = (f32[8,192,1]{1,0,2:T(8,128)S(1)}, f32[8,192,1]{1,0,2:T(8,128)S(1)}, u32[]{:S(2)}, u32[]{:S(2)}) collective-permute-start(f32[8,192,1]{1,0,2:T(8,128)S(1)} %copy.99), channel_id=1, source_target_pairs={{0,1},{1,2},{2,3},{3,4},{4,5},{5,6},{6,7},{7,0},{8,9},{9,10},{10,1... | collective-permute-start | bytes 18440 | tf_op jit(solution)/shard_map/ppermute | solution.py:17
  104.9 4.9 %collective-permute-start.9 = (f32[8,192,1]{1,0,2:T(8,128)S(1)}, f32[8,192,1]{1,0,2:T(8,128)S(1)}, u32[]{:S(2)}, u32[]{:S(2)}) collective-permute-start(f32[8,192,1]{1,0,2:T(8,128)S(1)} %copy.100), channel_id=1, source_target_pairs={{1,0},{2,1},{3,2},{4,3},{5,4},{6,5},{7,6},{0,7},{9,8},{10,9},{11,1... | collective-permute-start | bytes 18440 | tf_op jit(solution)/shard_map/ppermute | solution.py:19
  109.7 17.6 %copy-start.4 = (f32[8,192,1]{2,1,0:T(8,128)}, f32[8,192,1]{2,1,0:T(8,128)S(1)}, u32[]{:S(2)}) copy-start(f32[8,192,1]{2,1,0:T(8,128)S(1)} %copy.101) | copy-start | bytes 18436
  110.1 19.0 %copy-start.6 = (f32[8,192,1]{2,1,0:T(8,128)}, f32[8,192,1]{2,1,0:T(8,128)S(1)}, u32[]{:S(2)}) copy-start(f32[8,192,1]{2,1,0:T(8,128)S(1)} %copy.102) | copy-start | bytes 18436
  110.3 18.8 %collective-permute-start.11 = (f32[8,1,130]{2,0,1:T(8,128)S(1)}, f32[8,1,130]{2,0,1:T(8,128)S(1)}, u32[]{:S(2)}, u32[]{:S(2)}) collective-permute-start(f32[8,1,130]{2,0,1:T(8,128)S(1)} %copy.123), channel_id=1, source_target_pairs={{8,0},{16,8},{24,16},{9,1},{17,9},{25,17},{10,2},{18,10},{26,18},{... | collective-permute-start | bytes 12488 | tf_op jit(solution)/shard_map/ppermute | solution.py:19
  111.6 17.5 %collective-permute-start.10 = (f32[8,1,130]{2,0,1:T(8,128)S(1)}, f32[8,1,130]{2,0,1:T(8,128)S(1)}, u32[]{:S(2)}, u32[]{:S(2)}) collective-permute-start(f32[8,1,130]{2,0,1:T(8,128)S(1)} %copy.103), channel_id=1, source_target_pairs={{0,8},{8,16},{16,24},{1,9},{9,17},{17,25},{2,10},{10,18},{18,26},{... | collective-permute-start | bytes 12488 | tf_op jit(solution)/shard_map/ppermute | solution.py:17
  132.7 43.0 %copy-start.18 = (f32[8]{0:T(128)S(1)}, f32[8]{0:T(128)}, u32[]{:S(2)}) copy-start(f32[8]{0:T(128)} %copy-done.17) | copy-start | bytes 100
  132.7 43.0 %copy-start.20 = (f32[8]{0:T(128)S(1)}, f32[8]{0:T(128)}, u32[]{:S(2)}) copy-start(f32[8]{0:T(128)} %copy-done.19) | copy-start | bytes 100
  179.7 4.9 %collective-permute-start.12 = (f32[8,192,1]{1,0,2:T(8,128)S(1)}, f32[8,192,1]{1,0,2:T(8,128)S(1)}, u32[]{:S(2)}, u32[]{:S(2)}) collective-permute-start(f32[8,192,1]{1,0,2:T(8,128)S(1)} %copy.109), channel_id=1, source_target_pairs={{0,1},{1,2},{2,3},{3,4},{4,5},{5,6},{6,7},{7,0},{8,9},{9,10},{10,1... | collective-permute-start | bytes 18440 | tf_op jit(solution)/shard_map/ppermute | solution.py:17
  180.1 4.9 %collective-permute-start.13 = (f32[8,192,1]{1,0,2:T(8,128)S(1)}, f32[8,192,1]{1,0,2:T(8,128)S(1)}, u32[]{:S(2)}, u32[]{:S(2)}) collective-permute-start(f32[8,192,1]{1,0,2:T(8,128)S(1)} %copy.110), channel_id=1, source_target_pairs={{1,0},{2,1},{3,2},{4,3},{5,4},{6,5},{7,6},{0,7},{9,8},{10,9},{11,1... | collective-permute-start | bytes 18440 | tf_op jit(solution)/shard_map/ppermute | solution.py:19
  184.9 17.6 %copy-start.3 = (f32[8,192,1]{2,1,0:T(8,128)}, f32[8,192,1]{2,1,0:T(8,128)S(1)}, u32[]{:S(2)}) copy-start(f32[8,192,1]{2,1,0:T(8,128)S(1)} %copy.111) | copy-start | bytes 18436
  185.3 19.0 %copy-start.5 = (f32[8,192,1]{2,1,0:T(8,128)}, f32[8,192,1]{2,1,0:T(8,128)S(1)}, u32[]{:S(2)}) copy-start(f32[8,192,1]{2,1,0:T(8,128)S(1)} %copy.112) | copy-start | bytes 18436
  185.4 18.8 %collective-permute-start.15 = (f32[8,1,130]{2,0,1:T(8,128)S(1)}, f32[8,1,130]{2,0,1:T(8,128)S(1)}, u32[]{:S(2)}, u32[]{:S(2)}) collective-permute-start(f32[8,1,130]{2,0,1:T(8,128)S(1)} %copy.124), channel_id=1, source_target_pairs={{8,0},{16,8},{24,16},{9,1},{17,9},{25,17},{10,2},{18,10},{26,18},{... | collective-permute-start | bytes 12488 | tf_op jit(solution)/shard_map/ppermute | solution.py:19
  186.7 17.6 %collective-permute-start.14 = (f32[8,1,130]{2,0,1:T(8,128)S(1)}, f32[8,1,130]{2,0,1:T(8,128)S(1)}, u32[]{:S(2)}, u32[]{:S(2)}) collective-permute-start(f32[8,1,130]{2,0,1:T(8,128)S(1)} %copy.113), channel_id=1, source_target_pairs={{0,8},{8,16},{16,24},{1,9},{9,17},{17,25},{2,10},{10,18},{18,26},{... | collective-permute-start | bytes 12488 | tf_op jit(solution)/shard_map/ppermute | solution.py:17
  207.8 42.9 %copy-start.13 = (f32[8]{0:T(128)S(1)}, f32[8]{0:T(128)}, u32[]{:S(2)}) copy-start(f32[8]{0:T(128)} %copy-done.12) | copy-start | bytes 100
  207.8 42.9 %copy-start.14 = (f32[8]{0:T(128)S(1)}, f32[8]{0:T(128)}, u32[]{:S(2)}) copy-start(f32[8]{0:T(128)} %get-tuple-element.67) | copy-start | bytes 100
  207.9 42.9 %copy-start.2 = (f32[8,192,128]{2,1,0:T(8,128)S(1)}, f32[8,192,128]{2,1,0:T(8,128)}, u32[]{:S(2)}) copy-start(f32[8,192,128]{2,1,0:T(8,128)} %copy-done.1) | copy-start | bytes 2359300
  207.9 42.9 %copy-start.11 = (f32[8]{0:T(128)S(1)}, f32[8]{0:T(128)}, u32[]{:S(2)}) copy-start(f32[8]{0:T(128)} %copy-done.10) | copy-start | bytes 100
  207.9 42.9 %copy-start.16 = (f32[8]{0:T(128)S(1)}, f32[8]{0:T(128)}, u32[]{:S(2)}) copy-start(f32[8]{0:T(128)} %copy-done.15) | copy-start | bytes 100
  (5 other events, 12.3 us)
where the time goes:
time: 255 us; the launch traced here: 254 us
  blocking collectives  166 us (65%)
  starting transfers between devices  30.2 us (12%)
  other arithmetic  29.4 us (12%)
  local copies, waits for them, and re-layouts  23 us (9%)
  waiting for transfers between devices  4.77 us (2%)
    psum x3, blocking collectives, paired_sums(): lax.psum((jnp.sum(residual * scaled, axis=(1, 2)), jnp.sum(scaled * image...  119 us
    all_gather x3, blocking collectives, operate(): whole_top = lax.all_gather(top_row, 'lon', axis=1, tiled=True)  33.6 us
    ppermute x8, starting transfers between devices, extended(): lax.ppermute(tail, axis, [(i, (i + 1) % count) for i in range(ends)])  15.2 us
    ppermute x8, starting transfers between devices, extended(): lax.ppermute(head, axis, [((i + 1) % count, i) for i in range(ends)])  15 us
    all_gather x1, blocking collectives, body(): whole_north = lax.all_gather(north_top, 'lon', axis=0, tiled=True)  13.4 us
    reduce_sum x3, other arithmetic, paired_sums(): jnp.sum(scaled * image, axis=(1, 2))  9.31 us
  transfers between devices with their start and end apart: 16, of which 4 were waited for; matrix products, arithmetic and copies ran while one was open for 7% of the time, Pallas kernels for 0%

commit v1 on v0

v1 whole, which is shorter than its diff:
```python
import jax
import jax.numpy as jnp
from jax import lax
from jax.experimental import pallas as pl
from jax.experimental.pallas import tpu as pltpu
from jax.sharding import PartitionSpec as P

ITERS = 3
DEPTH = ITERS
SUB = 8
TOP = 2 * SUB


def pack_kernel(rhs, center, couplings, land, east, west, north, south):
    members = rhs.shape[0]
    fields = members + couplings.shape[0] + 1
    rows, cols = center.shape
    lane = lax.broadcasted_iota(jnp.int32, (SUB, cols), 1)
    group = 2 * DEPTH

    def chunk_fields(at):
        weight = land[pl.ds(at, SUB), :].astype(jnp.float32) / center[pl.ds(at, SUB), :]
        out = [rhs[m, pl.ds(at, SUB), :] * weight for m in range(members)]
        out += [couplings[c, pl.ds(at, SUB), :] for c in range(couplings.shape[0])]
        return out + [weight]

    def step(index, carry):
        at = pl.multiple_of(index * SUB, SUB)
        values = chunk_fields(at)
        to_east = jnp.zeros((SUB, cols), jnp.float32)
        to_west = jnp.zeros((SUB, cols), jnp.float32)
        for f, value in enumerate(values):
            base = group * f
            moved = pltpu.roll(value, (base + DEPTH) % cols, 1)
            pick_east = jnp.logical_and(lane >= base, lane < base + DEPTH)
            pick_west = jnp.logical_and(lane >= base + DEPTH, lane < base + group)
            to_east = jnp.where(pick_east, moved, to_east)
            to_west = jnp.where(pick_west, moved, to_west)
        east[pl.ds(at, SUB), :] = to_east
        west[pl.ds(at, SUB), :] = to_west
        return carry

    lax.fori_loop(0, rows // SUB, step, 0)
    for ref, at, first in ((north, rows - SUB, SUB - DEPTH), (south, 0, 0)):
        for f, value in enumerate(chunk_fields(at)):
            ref[DEPTH * f : DEPTH * (f + 1), :] = value[first : first + DEPTH, :]
        used = DEPTH * fields
        ref[used:, :] = jnp.zeros((ref.shape[0] - used, cols), jnp.float32)


def stencil_kernel(
    partner, rhs, center, couplings, land, from_west, from_east, from_north, from_south, ring,
    first, second, third, moments, held, coeff, level_one, level_two,
):
    members = rhs.shape[0]
    edges = couplings.shape[0]
    fields = members + edges + 1
    rows, cols = center.shape
    group = 2 * DEPTH
    wide = 2 * cols
    blocks = ring.shape[0]
    packed = ring.shape[1]
    f_east, f_north, f_ne, f_nw, f_weight = (members + c for c in range(5))
    lat_last = lax.axis_index("lat") == lax.axis_size("lat") - 1
    first_col = lax.axis_index("lon") * cols
    lane = lax.broadcasted_iota(jnp.int32, (SUB, cols), 1)
    in_west = lane % group < DEPTH
    bottom = TOP + rows

    zeros = jnp.zeros((SUB, wide), jnp.float32)
    for at in (0, SUB, bottom, bottom + SUB):
        for f in range(fields):
            held[f, at : at + SUB, :] = zeros
    for at in (0, bottom + SUB):
        for m in range(members):
            level_one[m, at : at + SUB, :] = zeros
            level_two[m, at : at + SUB, :] = zeros

    def spread(value, f):
        return pltpu.roll(value, (cols - group * f - DEPTH) % cols, 1)

    def fill(index, carry):
        at = pl.multiple_of(index * SUB, SUB)
        to = pl.multiple_of(index * SUB + TOP, SUB)
        weight = land[pl.ds(at, SUB), :].astype(jnp.float32) / center[pl.ds(at, SUB), :]
        side = jnp.where(in_west, from_west[pl.ds(at, SUB), :], from_east[pl.ds(at, SUB), :])
        for f in range(fields):
            if f < members:
                value = rhs[f, pl.ds(at, SUB), :] * weight
            elif f < f_weight:
                value = couplings[f - members, pl.ds(at, SUB), :]
            else:
                value = weight
            held[f, pl.ds(to, SUB), :cols] = value
            held[f, pl.ds(to, SUB), cols:] = spread(side, f)
        return carry

    lax.fori_loop(0, rows // SUB, fill, 0)

    side_south = from_south[packed : packed + SUB, :]
    for f in range(fields):
        held[f, TOP - DEPTH : TOP, :cols] = from_south[DEPTH * f : DEPTH * (f + 1), :]
        held[f, TOP - DEPTH : TOP, cols:] = spread(side_south, f)[SUB - DEPTH :, :]

    @pl.when(jnp.logical_not(lat_last))
    def _():
        side_north = from_north[packed : packed + SUB, :]
        for f in range(fields):
            held[f, bottom : bottom + DEPTH, :cols] = from_north[DEPTH * f : DEPTH * (f + 1), :]
            held[f, bottom : bottom + DEPTH, cols:] = spread(side_north, f)[:DEPTH, :]

    @pl.when(lat_last)
    def _():
        total = blocks * cols
        shift = cols.bit_length() - 1
        row = lax.broadcasted_iota(jnp.int32, (packed, cols), 0)
        spot = lax.broadcasted_iota(jnp.int32, (packed, cols), 1)

        def of(f):
            return jnp.logical_and(row >= DEPTH * f, row < DEPTH * (f + 1))

        offset = jnp.where(jnp.logical_or(of(f_east), of(f_ne)), -1, jnp.where(of(f_nw), 1, 0))
        beside = jnp.where(spot < cols // 2, spot + cols, spot - cols)
        mirrored = []
        for column in (spot, beside):
            source = partner[0] - first_col + offset - column
            source = jnp.where(source < 0, source + total, source)
            source = jnp.where(source < 0, source + total, source)
            source = jnp.where(source >= total, source - total, source)
            block = lax.shift_right_logical(source, shift)
            place = jnp.bitwise_and(source, cols - 1)
            found = jnp.zeros((packed, cols), jnp.float32)
            for b in range(blocks):
                taken = jnp.take_along_axis(ring[b], place, axis=1, mode="promise_in_bounds")
                found = jnp.where(block == b, taken, found)
            mirrored.append(found)
        for half, found in enumerate(mirrored):
            lanes = slice(half * cols, (half + 1) * cols)
            for f in range(fields):
                back = 2 if f in (f_north, f_ne, f_nw) else 1
                for k in range(DEPTH):
                    at = DEPTH - back - k
                    if at >= 0:
                        spot_row = DEPTH * f + at
                        held[f, bottom + k : bottom + k + 1, lanes] = found[spot_row : spot_row + 1, :]
            top = slice(bottom - 1, bottom)
            across = found[DEPTH * f_north + DEPTH - 1 : DEPTH * (f_north + 1), :]
            held[f_north, top, lanes] = 0.5 * (held[f_north, top, lanes] + across)
            held[f_ne, top, lanes] = jnp.zeros((1, cols), jnp.float32)
            held[f_nw, top, lanes] = jnp.zeros((1, cols), jnp.float32)

    def east_of(value):
        return pltpu.roll(value, wide - 1, 1)

    def west_of(value):
        return pltpu.roll(value, 1, 1)

    def around(ref, at):
        return ref.at[:, pl.ds(pl.multiple_of(at - SUB, SUB), 3 * SUB), :]

    def make_coeff(index, carry):
        at = pl.multiple_of(index * SUB, SUB)
        here = pl.ds(at, SUB)
        near = around(held, at)
        weight = held[f_weight, here, :]
        weight_east = east_of(weight)
        weight_west = west_of(weight)
        coeff[0, here, :] = west_of(weight * held[f_east, here, :])
        coeff[1, here, :] = west_of(weight * held[f_ne, here, :])
        coeff[2, here, :] = weight_west * near[f_nw, SUB - 1 : 2 * SUB - 1, :]
        coeff[3, here, :] = weight_east * held[f_east, here, :]
        coeff[4, here, :] = east_of(weight * held[f_nw, here, :])
        coeff[5, here, :] = weight_east * near[f_ne, SUB - 1 : 2 * SUB - 1, :]
        coeff[6, here, :] = weight * held[f_north, here, :]
        coeff[7, here, :] = weight * near[f_north, SUB - 1 : 2 * SUB - 1, :]
        return carry

    chunks = rows // SUB
    lax.fori_loop(1, chunks + 3, make_coeff, 0)

    def level(source, target, result):
        def chunk(index, carry, inside):
            at = pl.multiple_of(index * SUB, SUB)
            here = pl.ds(at, SUB)
            c = [coeff[k, here, :] for k in range(8)]
            if inside:
                inner = pl.ds(pl.multiple_of(at - TOP, SUB), SUB)
                scale = center[inner, :]
            sums = []
            near = around(source, at)
            for m in range(members):
                mid = source[m, here, :]
                up = near[m, SUB + 1 : 2 * SUB + 1, :]
                down = near[m, SUB - 1 : 2 * SUB - 1, :]
                new = c[6] * up + c[7] * down
                new = new + east_of(c[0] * mid + c[1] * up + c[2] * down)
                new = new + west_of(c[3] * mid + c[4] * up + c[5] * down)
                if target is not None:
                    target[m, here, :] = new
                if inside:
                    kept = new[:, :cols]
                    result[m, inner, :] = kept
                    scaled = scale * mid[:, :cols]
                    sums.append(carry[2 * m] + scaled * mid[:, :cols])
                    sums.append(carry[2 * m + 1] + scaled * kept)
            return tuple(sums) if inside else carry

        start = tuple(jnp.zeros((SUB, cols), jnp.float32) for _ in range(2 * members))
        if target is not None:
            chunk(1, 0, False)
        out = lax.fori_loop(2, chunks + 2, lambda i, s: chunk(i, s, True), start)
        if target is not None:
            chunk(chunks + 2, 0, False)
        return out

    totals = [level(held, level_one, first), level(level_one, level_two, second), level(level_two, None, third)]
    out_row = lax.broadcasted_iota(jnp.int32, (SUB, cols), 0)
    tile = jnp.zeros((SUB, cols), jnp.float32)
    for k in range(2 * DEPTH):
        gathered = jnp.zeros((SUB, cols), jnp.float32)
        for m in range(members):
            one = jnp.sum(totals[k // 2][2 * m + k % 2], axis=0, keepdims=True)
            gathered = jnp.where(out_row == m, one, gathered)
        tile = jnp.where(lane == k, jnp.sum(gathered, axis=1, keepdims=True), tile)
    moments[...] = tile


def combine_kernel(moments, rhs, center, land, first, second, third, solution, residual):
    def inner(p, q):
        total = 0.0
        for i, a in enumerate(p):
            for j, b in enumerate(q):
                total = total + a * b * nu[i + j]
        return total

    nu = [moments[:, k : k + 1] for k in range(2 * DEPTH)]
    one = jnp.ones_like(nu[0])
    scaled = [one]
    direction = [one]
    answer = [jnp.zeros_like(one)] * DEPTH
    gamma = nu[0]
    for iteration in range(DEPTH):
        image = [d - e for d, e in zip(direction + [0.0], [0.0] + direction)]
        step = gamma / inner(direction, image)
        for i, d in enumerate(direction):
            answer[i] = answer[i] + step * d
        scaled = [z - step * q for z, q in zip(scaled + [0.0], image)]
        if iteration + 1 < DEPTH:
            gamma_next = inner(scaled, scaled)
            ratio = gamma_next / gamma
            direction = [z + ratio * d for z, d in zip(scaled, direction + [0.0])]
            gamma = gamma_next

    rows, cols = center.shape
    members = rhs.shape[0]
    wide_answer = [jnp.broadcast_to(a, (members, cols)) for a in answer]
    wide_scaled = [jnp.broadcast_to(a, (members, cols)) for a in scaled]

    def chunk(index, carry):
        here = pl.ds(pl.multiple_of(index * SUB, SUB), SUB)
        scale = center[here, :]
        weight = land[here, :].astype(jnp.float32) / scale
        for m in range(members):
            basis = [rhs[m, here, :] * weight, first[m, here, :], second[m, here, :], third[m, here, :]]
            got = sum(a[m : m + 1, :] * v for a, v in zip(wide_answer, basis))
            left = sum(a[m : m + 1, :] * v for a, v in zip(wide_scaled, basis))
            solution[m, here, :] = got
            residual[m, here, :] = scale * left
        return carry

    lax.fori_loop(0, rows // SUB, chunk, 0)


def shifted(value, axis, by, closed):
    count = lax.axis_size(axis)
    pairs = [(i, (i + by) % count) for i in range(count) if closed or 0 <= i + by < count]
    return lax.ppermute(value, axis, pairs)


def body(right_side, center, couplings, land_sea, fold_partner):
    members, rows, cols = right_side.shape
    fields = members + couplings.shape[0] + 1
    packed = -(-DEPTH * fields // SUB) * SUB
    f32 = jnp.float32
    vmem = pl.BlockSpec(memory_space=pltpu.VMEM)
    smem = pl.BlockSpec(memory_space=pltpu.SMEM)
    params = pltpu.CompilerParams(vmem_limit_bytes=32 * 1024 * 1024)

    def shape(*dims):
        return jax.ShapeDtypeStruct(dims, f32)

    east, west, north, south = pl.pallas_call(
        pack_kernel,
        in_specs=[vmem] * 4,
        out_specs=[vmem] * 4,
        out_shape=[shape(rows, cols), shape(rows, cols), shape(packed, cols), shape(packed, cols)],
        compiler_params=params,
        name="pack",
    )(right_side, center, couplings, land_sea)

    from_west = shifted(east, "lon", 1, True)
    from_east = shifted(west, "lon", -1, True)
    ring = lax.all_gather(north, "lon", axis=0, tiled=False)
    in_west = (lax.broadcasted_iota(jnp.int32, (SUB, cols), 1) % (2 * DEPTH)) < DEPTH
    upper = jnp.where(in_west, from_west[rows - SUB :], from_east[rows - SUB :])
    lower = jnp.where(in_west, from_west[:SUB], from_east[:SUB])
    from_south = shifted(jnp.concatenate([north, upper]), "lat", 1, False)
    from_north = shifted(jnp.concatenate([south, lower]), "lat", -1, False)

    tall = rows + 2 * TOP
    first, second, third, moments = pl.pallas_call(
        stencil_kernel,
        in_specs=[smem] + [vmem] * 9,
        out_specs=[vmem] * 4,
        out_shape=[shape(members, rows, cols)] * 3 + [shape(SUB, cols)],
        scratch_shapes=[
            pltpu.VMEM((fields, tall, 2 * cols), f32),
            pltpu.VMEM((8, tall, 2 * cols), f32),
            pltpu.VMEM((members, tall, 2 * cols), f32),
            pltpu.VMEM((members, tall, 2 * cols), f32),
        ],
        compiler_params=params,
        name="stencil",
    )(fold_partner, right_side, center, couplings, land_sea, from_west, from_east, from_north, from_south, ring)

    for axis in ("lon", "lat"):
        count = lax.axis_size(axis)
        span = 1
        while span < count:
            moments = moments + lax.ppermute(moments, axis, [(i, i ^ span) for i in range(count)])
            span *= 2

    return tuple(
        pl.pallas_call(
            combine_kernel,
            in_specs=[vmem] * 7,
            out_specs=[vmem] * 2,
            out_shape=[shape(members, rows, cols)] * 2,
            compiler_params=params,
            name="combine",
        )(moments, right_side, center, land_sea, first, second, third)
    )


def solution(mesh):
    return jax.shard_map(
        body,
        mesh=mesh,
        in_specs=(
            P(None, "lat", "lon"),
            P("lat", "lon"),
            P(None, "lat", "lon"),
            P("lat", "lon"),
            P(),
        ),
        out_specs=(P(None, "lat", "lon"), P(None, "lat", "lon")),
        check_vma=False,
    )
```

time: 255 us -> 68.7 us (0.27)
  blocking collectives: 166 us -> 14 us
  other arithmetic: 29.4 us -> 0.05 us
  Pallas kernels: 0 us -> 19.5 us
  local copies, waits for them, and re-layouts: 23 us -> 3.92 us
  starting transfers between devices: 30.2 us -> 16.5 us
  waiting for transfers between devices: 4.77 us -> 13.7 us
    psum x3 -> x0, blocking collectives: 119 us -> none  [paired_sums(): lax.psum((jnp.sum(residual * scaled, axis=(1, 2)), jnp.sum(scaled * image...]
    all_gather x4 -> x1, blocking collectives: 47.1 us -> 14 us  [body(): ring = lax.all_gather(north, 'lon', axis=0, tiled=False)]
    pallas_call x0 -> x3, Pallas kernels: none -> 19.5 us  [the longest x1 14.2 us: body(): pl.pallas_call(stencil_kernel, in_specs=[smem] + [vmem] * 9, out_specs=[v...]
    ppermute x16 -> x9, starting transfers between devices: 30.2 us -> 16.5 us  [the longest x4 9.87 us: shifted(): return lax.ppermute(value, axis, pairs)]
    reduce_sum x3 -> x0, other arithmetic: 9.31 us -> none  [paired_sums(): jnp.sum(scaled * image, axis=(1, 2))]
    ppermute x16 -> x9, waiting for transfers between devices: 4.77 us -> 13.7 us  [the longest x5 11.4 us: body(): lax.ppermute(moments, axis, [(i, i ^ span) for i in range(count)])]
    slice x16 -> x0, local copies, waits for them, and re-layouts: 6.58 us -> none  [the longest x9 3.67 us: extended(): lax.slice_in_dim(cells, cells.shape[dim] - width, cells.shape[dim], axis=...]
    div x6 -> x0, other arithmetic: 5.51 us -> none  [the longest x3 4.9 us: body(): scaled = residual / center]
  transfers between devices with their start and end apart: 16 -> 9, of which waited for: 4 -> 6; matrix products, arithmetic and copies ran while one was open for 7% -> 0% of each run, Pallas kernels for 0% -> 0%
where the time goes in v1:
time: 68.7 us; the launch traced here: 68.4 us
  Pallas kernels  19.5 us (28%)
  starting transfers between devices  16.5 us (24%)
  blocking collectives  14 us (20%)
  waiting for transfers between devices  13.7 us (20%)
  local copies, waits for them, and re-layouts  3.92 us (6%)
  between operations  0.72 us (1%)
    pallas_call x1, Pallas kernels, body(): pl.pallas_call(stencil_kernel, in_specs=[smem] + [vmem] * 9, out_specs=[v...  14.2 us
    all_gather x1, blocking collectives, body(): ring = lax.all_gather(north, 'lon', axis=0, tiled=False)  14 us
    ppermute x5, waiting for transfers between devices, body(): lax.ppermute(moments, axis, [(i, i ^ span) for i in range(count)])  11.4 us
    ppermute x4, starting transfers between devices, shifted(): return lax.ppermute(value, axis, pairs)  9.87 us
    ppermute x5, starting transfers between devices, body(): lax.ppermute(moments, axis, [(i, i ^ span) for i in range(count)])  6.6 us
    unnamed x12, local copies, waits for them, and re-layouts  3.92 us
    pallas_call x1, Pallas kernels, body(): pl.pallas_call(combine_kernel, in_specs=[vmem] * 7, out_specs=[vmem] * 2,...  3.06 us
    ppermute x4, waiting for transfers between devices, shifted(): return lax.ppermute(value, axis, pairs)  2.27 us
  transfers between devices with their start and end apart: 9, of which 6 were waited for; matrix products, arithmetic and copies ran while one was open for 0% of the time, Pallas kernels for 0%

profile of v1, /device:TPU:0, one launch (start us, length us, event | category | flops | bytes accessed | tf_op | source)
XLA Modules:
  0.0 68.4 jit_solution(7858562795023897386)
XLA Ops:
  0.6 0.0 copy-start
  0.6 1.1 %copy-done = f32[8,192,128]{2,1,0:T(8,128)S(1)} copy-done((f32[8,192,128]{2,1,0:T(8,128)S(1)}, f32[8,192,128]{2,1,0:T(8,128)}, u32[]{:S(2)}) %copy-start) | copy-done | bytes 786456
  1.8 0.0 copy-start.1
  1.8 1.0 %copy-done.1 = f32[4,192,128]{2,1,0:T(8,128)S(1)} copy-done((f32[4,192,128]{2,1,0:T(8,128)S(1)}, f32[4,192,128]{2,1,0:T(8,128)}, u32[]{:S(2)}) %copy-start.1) | copy-done | bytes 393240
  2.8 0.9 %copy-done.2 = f32[192,128]{1,0:T(8,128)S(1)} copy-done((f32[192,128]{1,0:T(8,128)S(1)}, f32[192,128]{1,0:T(8,128)}, u32[]{:S(2)}) %copy-start.2) | copy-done | bytes 98328
  3.7 0.9 %copy-done.3 = s32[192,128]{1,0:T(8,128)S(1)} copy-done((s32[192,128]{1,0:T(8,128)S(1)}, s32[192,128]{1,0:T(8,128)}, u32[]{:S(2)}) %copy-start.3) | copy-done | bytes 98328
  4.5 2.2 %pack.1 = (f32[192,128]{1,0:T(8,128)S(1)}, f32[192,128]{1,0:T(8,128)S(1)}, f32[40,128]{1,0:T(8,128)S(1)}, f32[40,128]{1,0:T(8,128)S(1)}) custom-call(f32[8,192,128]{2,1,0:T(8,128)S(1)} %copy-done, f32[192,128]{1,0:T(8,128)S(1)} %copy-done.2, f32[4,192,128]{2,1,0:T(8,128)S(1)} %copy-done.1, s32[192,128]{1,0:T(8,128)S(1)} %copy-done.3), custom_call_target="tpu_custom_call" | custom-call | tf_op jit(solution)/shard_map/pack/pallas_call | solution.py:292
  6.8 0.5 collective-permute-start
  7.3 4.1 %collective-permute-start.1 = (f32[192,128]{1,0:T(8,128)S(1)}, f32[192,128]{1,0:T(8,128)S(1)}, u32[]{:S(2)}, u32[]{:S(2)}) collective-permute-start(f32[192,128]{1,0:T(8,128)S(1)} %get-tuple-element.11), channel_id=1, source_target_pairs={{0,7},{1,0},{2,1},{3,2},{4,3},{5,4},{6,5},{7,6},{8,15},{9,8},{10,9... | collective-permute-start | bytes 294920 | tf_op jit(solution)/shard_map/ppermute | solution.py:277
  11.4 2.3 %collective-permute-done.from_west = f32[192,128]{1,0:T(8,128)S(1)} collective-permute-done((f32[192,128]{1,0:T(8,128)S(1)}, f32[192,128]{1,0:T(8,128)S(1)}, u32[]{:S(2)}, u32[]{:S(2)}) %collective-permute-start) | collective-permute-done | bytes 98336 | tf_op jit(solution)/shard_map/ppermute | solution.py:277
  13.7 0.0 collective-permute-done.1.from_east
  13.7 3.9 %collective-permute-start.3 = (f32[48,128]{1,0:T(8,128)S(1)}, f32[48,128]{1,0:T(8,128)S(1)}, u32[]{:S(2)}, u32[]{:S(2)}) collective-permute-start(f32[48,128]{1,0:T(8,128)S(1)} %pad_maximum_fusion.1), channel_id=1, source_target_pairs={{0,8},{8,16},{16,24},{1,9},{9,17},{17,25},{2,10},{10,18},{18,26},{... | collective-permute-start | bytes 73736 | tf_op jit(solution)/shard_map/ppermute | solution.py:277
  17.7 1.3 %collective-permute-start.2 = (f32[48,128]{1,0:T(8,128)S(1)}, f32[48,128]{1,0:T(8,128)S(1)}, u32[]{:S(2)}, u32[]{:S(2)}) collective-permute-start(f32[48,128]{1,0:T(8,128)S(1)} %pad_maximum_fusion), channel_id=1, source_target_pairs={{8,0},{16,8},{24,16},{9,1},{17,9},{25,17},{10,2},{18,10},{26,18},{... | collective-permute-start | bytes 73736 | tf_op jit(solution)/shard_map/ppermute | solution.py:277
  19.0 0.0 copy-start.5
  19.0 14.0 %all-gather = f32[320,128]{1,0:T(8,128)S(1)} all-gather(f32[40,128]{1,0:T(8,128)S(1)} %get-tuple-element.13), channel_id=2, replica_groups=mesh['lat'=4,'lon'=8] {'lon'}, dimensions={0}, use_global_device_ids=true | all-gather | bytes 184320 | tf_op jit(solution)/shard_map/all_gather | solution.py:303
  33.0 0.0 collective-permute-done.3.from_south
  33.0 0.0 collective-permute-done.2.from_north
  33.0 0.0 copy-done.5
  33.0 0.0 copy-start.4
  33.0 14.2 %stencil.1 = (f32[8,192,128]{2,1,0:T(8,128)S(1)}, f32[8,192,128]{2,1,0:T(8,128)S(1)}, f32[8,192,128]{2,1,0:T(8,128)S(1)}, f32[8,128]{1,0:T(8,128)S(1)}) custom-call(s32[1024]{0:T(1024)S(1)} %copy-done.5, f32[8,192,128]{2,1,0:T(8,128)S(1)} %copy-done, f32[192,128]{1,0:T(8,128)S(1)} %copy-done.2, f32[4,192,128]{2,1,0:T(8,128)S(1)} %copy-done.1, ...), custom_call_target="tpu_custom_call" | custom-call | tf_op jit(solution)/shard_map/stencil/pallas_call | solution.py:311
  47.3 0.4 collective-permute-start.4
  47.6 0.8 %collective-permute-done.4 = f32[8,128]{1,0:T(8,128)S(1)} collective-permute-done((f32[8,128]{1,0:T(8,128)S(1)}, f32[8,128]{1,0:T(8,128)S(1)}, u32[]{:S(2)}, u32[]{:S(2)}) %collective-permute-start.4) | collective-permute-done | bytes 4128 | tf_op jit(solution)/shard_map/ppermute | solution.py:330
  48.5 0.1 collective-permute-start.5
  48.5 3.5 %collective-permute-done.5 = f32[8,128]{1,0:T(8,128)S(1)} collective-permute-done((f32[8,128]{1,0:T(8,128)S(1)}, f32[8,128]{1,0:T(8,128)S(1)}, u32[]{:S(2)}, u32[]{:S(2)}) %collective-permute-start.5) | collective-permute-done | bytes 4128 | tf_op jit(solution)/shard_map/ppermute | solution.py:330
  52.1 0.6 collective-permute-start.6
  52.7 3.9 %collective-permute-done.6 = f32[8,128]{1,0:T(8,128)S(1)} collective-permute-done((f32[8,128]{1,0:T(8,128)S(1)}, f32[8,128]{1,0:T(8,128)S(1)}, u32[]{:S(2)}, u32[]{:S(2)}) %collective-permute-start.6) | collective-permute-done | bytes 4128 | tf_op jit(solution)/shard_map/ppermute | solution.py:330
  56.6 2.6 %collective-permute-start.7 = (f32[8,128]{1,0:T(8,128)S(1)}, f32[8,128]{1,0:T(8,128)S(1)}, u32[]{:S(2)}, u32[]{:S(2)}) collective-permute-start(f32[8,128]{1,0:T(8,128)S(1)} %add.27), channel_id=1, source_target_pairs={{0,8},{8,0},{16,24},{24,16},{1,9},{9,1},{17,25},{25,17},{2,10},{10... | collective-permute-start | bytes 12296 | tf_op jit(solution)/shard_map/ppermute | solution.py:330
  59.2 1.6 %collective-permute-done.7 = f32[8,128]{1,0:T(8,128)S(1)} collective-permute-done((f32[8,128]{1,0:T(8,128)S(1)}, f32[8,128]{1,0:T(8,128)S(1)}, u32[]{:S(2)}, u32[]{:S(2)}) %collective-permute-start.7) | collective-permute-done | bytes 4128 | tf_op jit(solution)/shard_map/ppermute | solution.py:330
  60.8 3.0 %collective-permute-start.8 = (f32[8,128]{1,0:T(8,128)S(1)}, f32[8,128]{1,0:T(8,128)S(1)}, u32[]{:S(2)}, u32[]{:S(2)}) collective-permute-start(f32[8,128]{1,0:T(8,128)S(1)} %add.28), channel_id=1, source_target_pairs={{0,16},{8,24},{16,0},{24,8},{1,17},{9,25},{17,1},{25,9},{2,18},{10... | collective-permute-start | bytes 12296 | tf_op jit(solution)/shard_map/ppermute | solution.py:330
  63.8 1.6 %collective-permute-done.8 = f32[8,128]{1,0:T(8,128)S(1)} collective-permute-done((f32[8,128]{1,0:T(8,128)S(1)}, f32[8,128]{1,0:T(8,128)S(1)}, u32[]{:S(2)}, u32[]{:S(2)}) %collective-permute-start.8) | collective-permute-done | bytes 4128 | tf_op jit(solution)/shard_map/ppermute | solution.py:330
  65.3 0.0 copy-done.4
  65.3 3.1 %combine.1 = (f32[8,192,128]{2,1,0:T(8,128)}, f32[8,192,128]{2,1,0:T(8,128)}) custom-call(f32[8,128]{1,0:T(8,128)S(1)} %add.29.moments, f32[8,192,128]{2,1,0:T(8,128)S(1)} %copy-done, f32[192,128]{1,0:T(8,128)S(1)} %copy-done.2, s32[192,128]{1,0:T(8,128)S(1)} %copy-done.4, f32[8,192,128]{2,1,0:T(8,128)S(1)} %get-tuple-element.15.first, ...), custom_call_target="tpu_custom_call" | custom-call | tf_op jit(solution)/shard_map/combine/pallas_call | solution.py:334
  (12 shorter events, 0.1 us)
Async XLA Ops:
  0.6 1.1 %copy-start = (f32[8,192,128]{2,1,0:T(8,128)S(1)}, f32[8,192,128]{2,1,0:T(8,128)}, u32[]{:S(2)}) copy-start(f32[8,192,128]{2,1,0:T(8,128)} %rhs.5) | copy-start | bytes 2359300
  1.8 1.0 %copy-start.1 = (f32[4,192,128]{2,1,0:T(8,128)S(1)}, f32[4,192,128]{2,1,0:T(8,128)}, u32[]{:S(2)}) copy-start(f32[4,192,128]{2,1,0:T(8,128)} %couplings.3) | copy-start | bytes 1179652
  2.8 0.9 %copy-start.2 = (f32[192,128]{1,0:T(8,128)S(1)}, f32[192,128]{1,0:T(8,128)}, u32[]{:S(2)}) copy-start(f32[192,128]{1,0:T(8,128)} %center.5) | copy-start | bytes 294916
  3.7 0.9 %copy-start.3 = (s32[192,128]{1,0:T(8,128)S(1)}, s32[192,128]{1,0:T(8,128)}, u32[]{:S(2)}) copy-start(s32[192,128]{1,0:T(8,128)} %land.5) | copy-start | bytes 294916
  6.8 6.9 %collective-permute-start = (f32[192,128]{1,0:T(8,128)S(1)}, f32[192,128]{1,0:T(8,128)S(1)}, u32[]{:S(2)}, u32[]{:S(2)}) collective-permute-start(f32[192,128]{1,0:T(8,128)S(1)} %get-tuple-element.10), channel_id=1, source_target_pairs={{0,1},{1,2},{2,3},{3,4},{4,5},{5,6},{6,7},{7,0},{8,9},{9,10},{10,1... | collective-permute-start | bytes 294920 | tf_op jit(solution)/shard_map/ppermute | solution.py:277
  7.3 6.4 %collective-permute-start.1 = (f32[192,128]{1,0:T(8,128)S(1)}, f32[192,128]{1,0:T(8,128)S(1)}, u32[]{:S(2)}, u32[]{:S(2)}) collective-permute-start(f32[192,128]{1,0:T(8,128)S(1)} %get-tuple-element.11), channel_id=1, source_target_pairs={{0,7},{1,0},{2,1},{3,2},{4,3},{5,4},{6,5},{7,6},{8,15},{9,8},{10,9... | collective-permute-start | bytes 294920 | tf_op jit(solution)/shard_map/ppermute | solution.py:277
  13.7 19.3 %collective-permute-start.3 = (f32[48,128]{1,0:T(8,128)S(1)}, f32[48,128]{1,0:T(8,128)S(1)}, u32[]{:S(2)}, u32[]{:S(2)}) collective-permute-start(f32[48,128]{1,0:T(8,128)S(1)} %pad_maximum_fusion.1), channel_id=1, source_target_pairs={{0,8},{8,16},{16,24},{1,9},{9,17},{17,25},{2,10},{10,18},{18,26},{... | collective-permute-start | bytes 73736 | tf_op jit(solution)/shard_map/ppermute | solution.py:277
  17.7 15.4 %collective-permute-start.2 = (f32[48,128]{1,0:T(8,128)S(1)}, f32[48,128]{1,0:T(8,128)S(1)}, u32[]{:S(2)}, u32[]{:S(2)}) collective-permute-start(f32[48,128]{1,0:T(8,128)S(1)} %pad_maximum_fusion), channel_id=1, source_target_pairs={{8,0},{16,8},{24,16},{9,1},{17,9},{25,17},{10,2},{18,10},{26,18},{... | collective-permute-start | bytes 73736 | tf_op jit(solution)/shard_map/ppermute | solution.py:277
  19.0 14.1 %copy-start.5 = (s32[1024]{0:T(1024)S(1)}, s32[1024]{0:T(1024)}, u32[]{:S(2)}) copy-start(s32[1024]{0:T(1024)} %partner.1) | copy-start | bytes 12292
  33.0 32.3 %copy-start.4 = (s32[192,128]{1,0:T(8,128)S(1)}, s32[192,128]{1,0:T(8,128)}, u32[]{:S(2)}) copy-start(s32[192,128]{1,0:T(8,128)} %land.5) | copy-start | bytes 294916
  47.3 1.2 %collective-permute-start.4 = (f32[8,128]{1,0:T(8,128)S(1)}, f32[8,128]{1,0:T(8,128)S(1)}, u32[]{:S(2)}, u32[]{:S(2)}) collective-permute-start(f32[8,128]{1,0:T(8,128)S(1)} %get-tuple-element.14), channel_id=1, source_target_pairs={{0,1},{1,0},{2,3},{3,2},{4,5},{5,4},{6,7},{7,6},{8,9},{9,8},{10,11... | collective-permute-start | bytes 12296 | tf_op jit(solution)/shard_map/ppermute | solution.py:330
  48.5 3.6 %collective-permute-start.5 = (f32[8,128]{1,0:T(8,128)S(1)}, f32[8,128]{1,0:T(8,128)S(1)}, u32[]{:S(2)}, u32[]{:S(2)}) collective-permute-start(f32[8,128]{1,0:T(8,128)S(1)} %add.25), channel_id=1, source_target_pairs={{0,2},{1,3},{2,0},{3,1},{4,6},{5,7},{6,4},{7,5},{8,10},{9,11},{10,... | collective-permute-start | bytes 12296 | tf_op jit(solution)/shard_map/ppermute | solution.py:330
  52.1 4.5 %collective-permute-start.6 = (f32[8,128]{1,0:T(8,128)S(1)}, f32[8,128]{1,0:T(8,128)S(1)}, u32[]{:S(2)}, u32[]{:S(2)}) collective-permute-start(f32[8,128]{1,0:T(8,128)S(1)} %add.26), channel_id=1, source_target_pairs={{0,4},{1,5},{2,6},{3,7},{4,0},{5,1},{6,2},{7,3},{8,12},{9,13},{10,... | collective-permute-start | bytes 12296 | tf_op jit(solution)/shard_map/ppermute | solution.py:330
  56.6 4.2 %collective-permute-start.7 = (f32[8,128]{1,0:T(8,128)S(1)}, f32[8,128]{1,0:T(8,128)S(1)}, u32[]{:S(2)}, u32[]{:S(2)}) collective-permute-start(f32[8,128]{1,0:T(8,128)S(1)} %add.27), channel_id=1, source_target_pairs={{0,8},{8,0},{16,24},{24,16},{1,9},{9,1},{17,25},{25,17},{2,10},{10... | collective-permute-start | bytes 12296 | tf_op jit(solution)/shard_map/ppermute | solution.py:330
  60.8 4.5 %collective-permute-start.8 = (f32[8,128]{1,0:T(8,128)S(1)}, f32[8,128]{1,0:T(8,128)S(1)}, u32[]{:S(2)}, u32[]{:S(2)}) collective-permute-start(f32[8,128]{1,0:T(8,128)S(1)} %add.28), channel_id=1, source_target_pairs={{0,16},{8,24},{16,0},{24,8},{1,17},{9,25},{17,1},{25,9},{2,18},{10... | collective-permute-start | bytes 12296 | tf_op jit(solution)/shard_map/ppermute | solution.py:330
